TPU v7x, 256 devices: a 8x8x2 block of a 8x8x16 slice. The times are simulated.
256 devices in a mesh: grp: 2 (over z), kv: 128 (over y, x, core).
Axes of the slice: x: 8, y: 8, z: 2, core: 2. Of those that a mesh axis runs over, the one named last changes fastest.
The devices are a block of a 8x8x16 slice.
Arguments:
- queries: bfloat16 [1024, 40, 128], P(('grp', 'kv')), parts along dimension 0, may hold values from -250 to 250
- cache_keys: bfloat16 [65536, 40, 128], P(('grp', 'kv')), parts along dimension 0, may hold values from -8 to 8
- cache_values: bfloat16 [65536, 40, 128], P(('grp', 'kv')), parts along dimension 0, may hold values from -18 to 18
- new_keys: bfloat16 [1024, 40, 128], P(('grp', 'kv')), parts along dimension 0, may hold values from -4 to 4
- new_values: bfloat16 [1024, 40, 128], P(('grp', 'kv')), parts along dimension 0, may hold values from -4 to 4
- valid_frames: int32 [2], P('grp'), parts along dimension 0, may hold values from 64 to 128
Outputs:
- attended: bfloat16 [1024, 40, 128], P(('grp', 'kv')), parts along dimension 0
There are 2 independent parts, one for each index of `grp`. A program takes and returns all parts, laid end to end along the dimension named above; each array names one. Nothing has to cross between parts.
All inputs are finite; a program needn't handle non-finite values.
Results may differ from a plain program's by a relative error of at most 0.0027.
Values may be sent and summed in bfloat16 or wider, within the bound.
A program may use at most 128 MiB of HBM per device.

v0:
```python
import functools
import math
import jax
import jax.numpy as jnp
from jax import lax
from jax.sharding import Mesh
from jax.sharding import PartitionSpec as P

FRAME = 256
QUERY_SPLIT = 4
KV = ("kv_0", "kv_1", "kv_2")
GRP_KV = ("grp", "kv_0", "kv_1", "kv_2")
masked_score = -1e30


def by_axis(x, axes):
    return functools.reduce(lax.pmax, axes, x)


def split_up(x, dim, peers):
    before, after = (x.shape[:dim], x.shape[dim + 1 :])
    return jnp.moveaxis(x.reshape(*before, peers, -1, *after), dim, 0)


def sum_packed(arrays, axis, dims):
    peers = lax.axis_size(axis)
    parts = [split_up(a, dim, peers) for a, dim in zip(arrays, dims)]
    lines = jnp.concatenate([b.reshape(peers, -1) for b in parts], axis=1)
    extent = max(16, -(-lines.shape[1] // 1024) * 8)
    lines = jnp.pad(lines, ((0, 0), (0, extent * 128 - lines.shape[1]))).reshape(-1, 128)
    line, at, done = (lax.psum_scatter(lines, axis, tiled=True).reshape(-1), 0, [])
    for b in parts:
        part = b[0]
        done.append(line[at : at + part.size].reshape(part.shape))
        at += part.size
    return tuple(done)


def per_device(queries, cache_keys, cache_values, new_keys, new_values, valid_frames):
    q_dev, heads, head_dim = queries.shape
    cache_dev = cache_keys.shape[0]
    factor = 1.0 / math.sqrt(head_dim)
    gathered = lax.all_gather(queries, KV, axis=0, tiled=True)
    devices = lax.axis_size(KV)
    position = lax.axis_index(KV) * cache_dev + lax.iota(jnp.int32, cache_dev)
    live = position < valid_frames[0] * FRAME
    per_block = q_dev // QUERY_SPLIT
    blocked = gathered.reshape(devices, QUERY_SPLIT, per_block, heads, head_dim)
    pieces = []
    half = heads // 2
    for index in range(QUERY_SPLIT):
        block = blocked[:, index].reshape(devices * per_block, heads, head_dim)
        halves = []
        for which in range(2):
            lower = which * half
            sub_block = block[:, lower : lower + half]
            ckeys = cache_keys[:, lower : lower + half]
            nkeys = new_keys[:, lower : lower + half]
            block_cache_score = (
                jnp.einsum("qhd,khd->hqk", sub_block, ckeys, preferred_element_type=jnp.float32)
                * factor
            )
            block_cache_score = jnp.where(
                live[None, None, :], block_cache_score, jnp.float32(masked_score)
            )
            block_new_score = (
                jnp.einsum("qhd,khd->hqk", sub_block, nkeys, preferred_element_type=jnp.float32)
                * factor
            )
            top = by_axis(
                jnp.maximum(jnp.max(block_cache_score, axis=2), jnp.max(block_new_score, axis=2)),
                KV,
            )
            cache_weight = jnp.exp(block_cache_score - top[:, :, None])
            new_weight = jnp.exp(block_new_score - top[:, :, None])
            total = jnp.sum(cache_weight, axis=2) + jnp.sum(new_weight, axis=2)
            numerator = jnp.einsum(
                "hqk,khd->qhd",
                cache_weight.astype(jnp.bfloat16),
                cache_values[:, lower : lower + half],
                preferred_element_type=jnp.float32,
            )
            numerator = numerator + jnp.einsum(
                "hqk,khd->qhd",
                new_weight.astype(jnp.bfloat16),
                new_values[:, lower : lower + half],
                preferred_element_type=jnp.float32,
            )
            numerator, total = (numerator, total.T)
            summed, denominator = sum_packed((numerator, total), KV, (0, 0))
            halves.append((summed / denominator[:, :, None]).astype(jnp.bfloat16))
        pieces.append(jnp.concatenate(halves, axis=1))
    return jnp.concatenate(pieces, axis=0)


def solution(mesh):
    torus = Mesh(mesh.devices.reshape(mesh.shape["grp"], 8, 8, 2), ("grp", "kv_0", "kv_1", "kv_2"))
    return jax.shard_map(
        per_device,
        mesh=torus,
        in_specs=(
            P(GRP_KV, None, None),
            P(GRP_KV, None, None),
            P(GRP_KV, None, None),
            P(GRP_KV, None, None),
            P(GRP_KV, None, None),
            P("grp"),
        ),
        out_specs=P(GRP_KV, None, None),
        check_vma=False,
    )
```

profile of v0, /device:TPU:518, one launch (start us, length us, event | category | flops | bytes accessed | tf_op | source)
XLA Modules:
  0.0 733.7 jit_solution(5114170117710780032)
XLA Ops:
  8.0 4.3 fusion.169
  14.4 2.8 copy.66
  17.2 4.3 fusion.170
  21.5 87.6 %all-gather.2.cloned.1.call-done = bf16[512,40,128]{2,1,0:T(8,128)(2,1)} async-done(((bf16[4,40,128]{2,1,0:T(8,128)(2,1)}), bf16[512,40,128]{2,1,0:T(8,128)(2,1)}) %all-gather.2.cloned.1.call-update) | async-done | bytes 5242896 | tf_op jit(solution)/shard_map/all_gather | solution.py:43
  109.1 3.6 fusion.168
  112.7 2.1 fusion.67
  116.9 2.1 fusion.69
  119.1 2.1 fusion.68
  129.4 2.3 fusion
  131.8 28.8 %pmax.168 = f32[20,128]{1,0:T(8,128)S(1)} all-reduce(f32[20,128]{1,0:T(8,128)S(1)} %max.72), channel_id=1, replica_groups=mesh['grp'=2,'kv_0'=8,'kv_1'=8,'kv_2'=2] {'kv_0'}, use_global_device_ids=true, to_apply=%region_2.3 | all-reduce | flops 2560 | bytes 20480 | tf_op jit(solution)/shard_map/pmax | solution.py:17
  160.6 26.6 %pmax.169 = f32[20,128]{1,0:T(8,128)S(1)} all-reduce(f32[20,128]{1,0:T(8,128)S(1)} %pmax.168), channel_id=1, replica_groups=mesh['grp'=2,'kv_0'=8,'kv_1'=8,'kv_2'=2] {'kv_1'}, use_global_device_ids=true, to_apply=%region_3.4 | all-reduce | flops 2560 | bytes 20480 | tf_op jit(solution)/shard_map/pmax | solution.py:17
  187.2 3.3 pmax.170
  190.5 10.1 %fusion.8 = (f32[20,128]{1,0:T(8,128)S(1)}, f32[20,128]{1,0:T(8,128)S(1)}, f32[20,128]{1,0:T(8,128)S(1)}, f32[20,128]{1,0:T(8,128)S(1)}, f32[20,128]{1,0:T(8,128...) fusion(f32[20,128,256]{2,1,0:T(8,128)} %get-tuple-element.62, ...), kind=kOutput, calls=%fused_computation.24 | convolution fusion | flops 184135680 | bytes 23685376 | tf_op jit(solution)/shard_map/qhd,khd->hqk/dot_general | solution.py:60
  205.2 3.6 convolution_add_fusion.7
  209.0 74.2 %all-reduce.29.cloned.1.call-done = (f32[20,128]{1,0:T(8,128)}, f32[20,128]{1,0:T(8,128)}, f32[20,128]{1,0:T(8,128)}, f32[20,128]{1,0:T(8,128)}, f32[20,128]{1,0...) async-done(((f32[20,128]{1,0:T(8,128)}, f32[20,128]{1,0:T(8,128)}, f32[20,128]{1,0:T(8,128)}, f32[20,128]{1,0:T(8,128)}, f32[20,128]{1,0:T(8,128)}, ...) | async-done | bytes 71696 | tf_op jit(solution)/shard_map/pmax | solution.py:17
  283.3 77.3 %all-reduce.27.cloned.1.call-done = (f32[20,128]{1,0:T(8,128)}, f32[20,128]{1,0:T(8,128)}, f32[20,128]{1,0:T(8,128)}, f32[20,128]{1,0:T(8,128)}, f32[20,128]{1,0...) async-done(((f32[20,128]{1,0:T(8,128)}, f32[20,128]{1,0:T(8,128)}, f32[20,128]{1,0:T(8,128)}, f32[20,128]{1,0:T(8,128)}, f32[20,128]{1,0:T(8,128)}, ...) | async-done | bytes 71696 | tf_op jit(solution)/shard_map/pmax | solution.py:17
  360.8 2.5 pad_maximum_fusion
  363.2 2.9 copy.75
  366.1 2.6 pad.25.clone
  368.8 2.6 reshape.131
  371.3 24.9 %all-reduce.31.cloned.1.call-done = (f32[20,128]{1,0:T(8,128)}, f32[20,128]{1,0:T(8,128)}, f32[20,128]{1,0:T(8,128)}, f32[20,128]{1,0:T(8,128)}, f32[20,128]{1,0...) async-done(((f32[20,128]{1,0:T(8,128)}, f32[20,128]{1,0:T(8,128)}, f32[20,128]{1,0:T(8,128)}, f32[20,128]{1,0:T(8,128)}, f32[20,128]{1,0:T(8,128)}, ...) | async-done | bytes 71696 | tf_op jit(solution)/shard_map/pmax | solution.py:17
  398.1 2.4 fusion.98
  408.2 8.6 %fusion.10 = (f32[20,128]{1,0:T(8,128)S(1)}, f32[20,128]{1,0:T(8,128)S(1)}, f32[20,128]{1,0:T(8,128)S(1)}, f32[20,128]{1,0:T(8,128)S(1)}, f32[20,128]{1,0:T(8,12...) fusion(f32[20,128,256]{2,1,0:T(8,128)} %get-tuple-element.65, f32[20,128]{1,0:T(8,128)S(1)} %copy-done.8, ...), kind=kLoop, calls=%fused_computation.26 | loop fusion | flops 18332160 | bytes 18493696 | tf_op jit(solution)/shard_map/reduce_sum | solution.py:76
  418.7 2.9 copy.82
  421.6 2.7 pad.32.clone
  424.2 2.6 reshape.145
  426.8 2.9 convolution_add_fusion.1
  430.9 2.8 copy.81
  433.8 2.6 pad.31.clone
  436.4 2.6 reshape.143
  439.0 2.9 convolution_add_fusion.2
  443.1 2.9 copy.80
  446.0 2.7 pad.30.clone
  448.7 2.6 reshape.141
  451.3 2.9 convolution_add_fusion.3
  455.3 2.9 copy.79
  458.2 2.7 pad.29.clone
  460.9 2.6 reshape.139
  463.5 2.9 convolution_add_fusion.4
  467.6 2.9 copy.78
  470.5 2.7 pad.28.clone
  473.2 2.6 reshape.137
  475.8 2.9 convolution_add_fusion.5
  479.8 2.8 copy.77
  482.7 2.7 pad.27.clone
  485.4 2.6 reshape.135
  488.0 2.5 convolution_add_fusion.6
  497.0 217.5 %all-reduce.25.cloned.1.call-done = (f32[3072,128]{1,0:T(8,128)}, f32[3072,128]{1,0:T(8,128)}, f32[3072,128]{1,0:T(8,128)}, f32[3072,128]{1,0:T(8,128)}, f32[307...) async-done(((f32[3072,128]{1,0:T(8,128)}, f32[3072,128]{1,0:T(8,128)}, f32[3072,128]{1,0:T(8,128)}, f32[3072,128]{1,0:T(8,128)}, ...) | async-done | bytes 12582928
  (126 shorter events, 54.2 us)
Async XLA Ops:
  6.5 102.6 %all-gather.2.cloned.1.call-start = ((), (), s32[]{:S(2)}) async-start(), calls=%async_computation | async-start | bytes 5283840 | tf_op jit(solution)/shard_map/all_gather | solution.py:43
  7.3 275.9 %all-reduce.29.cloned.1.call-start = ((), (), s32[]{:S(2)}) async-start(), calls=%async_computation.3 | async-start | bytes 172032 | tf_op jit(solution)/shard_map/pmax | solution.py:17
  14.4 2.8 copy-start.15
  14.4 2.8 copy-start.16
  109.1 3.6 copy-start.7
  112.7 2.1 copy-start.6
  200.6 4.6 copy-start
  208.9 151.8 %all-reduce.27.cloned.1.call-start = ((), (), s32[]{:S(2)}) async-start(), calls=%async_computation.2 | async-start | bytes 172032 | tf_op jit(solution)/shard_map/pmax | solution.py:17
  283.3 112.9 %all-reduce.31.cloned.1.call-start = ((), (), s32[]{:S(2)}) async-start(), calls=%async_computation.4 | async-start | bytes 172032 | tf_op jit(solution)/shard_map/pmax | solution.py:17
  360.7 353.8 %all-reduce.25.cloned.1.call-start = ((), (), s32[]{:S(2)}) async-start(), calls=%async_computation.1 | async-start | bytes 25165824
  396.2 4.3 copy-start.12
  396.2 4.3 copy-start.13
  398.1 4.0 copy-start.11
  398.1 10.1 %copy-start.3 = (f32[20,128,256]{2,1,0:T(8,128)S(1)}, f32[20,128,256]{2,1,0:T(8,128)}, u32[]{:S(2)}) copy-start(f32[20,128,256]{2,1,0:T(8,128)} %fusion.69) | copy-start | bytes 7864324
  400.4 3.1 copy-start.10
  402.1 3.0 copy-start.9
  402.1 6.1 copy-start.2
  403.5 3.0 copy-start.8
  405.1 3.1 copy-start.1
  405.1 3.1 copy-start.14
  408.1 8.6 %copy-start.4 = (f32[20,128,256]{2,1,0:T(8,128)S(1)}, f32[20,128,256]{2,1,0:T(8,128)}, u32[]{:S(2)}) copy-start(f32[20,128,256]{2,1,0:T(8,128)} %fusion.70) | copy-start | bytes 7864324
  485.4 2.7 copy-start.5
  495.0 0.7 copy-start.17
Sparse Core Ops, SparseCore 0:
  9.9 99.1 all-gather.1
  209.0 74.1 all-reduce.28
  286.1 74.4 all-reduce.26
  363.6 32.5 all-reduce.30
  495.2 219.2 all-reduce.24
where the time goes:
time: 736 us; the launch traced here: 734 us
  waiting for transfers between devices  482 us (65%)
  local copies, waits for them, and re-layouts  85.4 us (12%)
  matrix products  61.6 us (8%)
  blocking collectives  58.7 us (8%)
  other arithmetic  30.5 us (4%)
  between operations  14.8 us (2%)
    unnamed x6, waiting for transfers between devices  218 us
    pmax x3, waiting for transfers between devices, by_axis(): return functools.reduce(lax.pmax, axes, x)  176 us
    all_gather x1, waiting for transfers between devices, per_device(): gathered = lax.all_gather(queries, KV, axis=0, tiled=True)  87.6 us
    pmax x3, blocking collectives, by_axis(): return functools.reduce(lax.pmax, axes, x)  58.7 us
    unnamed x47, local copies, waits for them, and re-layouts  27.6 us
    dot_general x8, matrix products, per_device(): jnp.einsum('qhd,khd->hqk', sub_block, ckeys, preferred_element_type=jnp.f...  25 us
    dot_general x8, matrix products, per_device(): jnp.einsum('hqk,khd->qhd', cache_weight.astype(jnp.bfloat16), cache_value...  21.2 us
    pad x8, local copies, waits for them, and re-layouts, sum_packed(): jnp.pad(lines, ((0, 0), (0, extent * 128 - lines.shape[1])))  20.2 us
  transfers between devices with their start and end apart: 5, of which 5 were waited for; matrix products, arithmetic and copies ran while one was open for 3% of the time, Pallas kernels for 0%

commit v1 on v0

--- a/solution.py
+++ b/solution.py
@@ -40,7 +40,15 @@
     q_dev, heads, head_dim = queries.shape
     cache_dev = cache_keys.shape[0]
     factor = 1.0 / math.sqrt(head_dim)
-    gathered = lax.all_gather(queries, KV, axis=0, tiled=True)
+
+    def _fit_sites(incoming_x):
+        part_next = tuple((incoming_x for _ in range(lax.psum(1, KV))))
+        built = jnp.stack(part_next)
+        taken_in = lax.all_to_all(built, KV, 0, 0)
+        x_now = jnp.concatenate(taken_in, axis=0)
+        return x_now
+
+    gathered = _fit_sites(queries)
     devices = lax.axis_size(KV)
     position = lax.axis_index(KV) * cache_dev + lax.iota(jnp.int32, cache_dev)
     live = position < valid_frames[0] * FRAME

time: 736 us -> 822 us (1.12)
  waiting for transfers between devices: 482 us -> 519 us
  starting transfers between devices: 0.25 us -> 27.7 us
  blocking collectives: 58.7 us -> 75.3 us
    all_to_all x0 -> x1, waiting for transfers between devices: none -> 110 us  [_fit_sites(): taken_in = lax.all_to_all(built, KV, 0, 0)]
    all_gather x1 -> x0, waiting for transfers between devices: 87.6 us -> none  [per_device(): gathered = lax.all_gather(queries, KV, axis=0, tiled=True)]
    all_to_all x0 -> x1, starting transfers between devices: none -> 27.1 us  [_fit_sites(): taken_in = lax.all_to_all(built, KV, 0, 0)]
    pmax x3, blocking collectives: 58.7 us -> 75.3 us  [by_axis(): return functools.reduce(lax.pmax, axes, x)]
    pmax x3, waiting for transfers between devices: 176 us -> 192 us  [by_axis(): return functools.reduce(lax.pmax, axes, x)]
    unnamed x6 -> x5, waiting for transfers between devices: 218 us -> 218 us
    unnamed x47 -> x49, local copies, waits for them, and re-layouts: 27.6 us -> 26.9 us
where the time goes in v1:
time: 822 us; the launch traced here: 816 us
  waiting for transfers between devices  519 us (63%)
  local copies, waits for them, and re-layouts  87.6 us (11%)
  blocking collectives  75.3 us (9%)
  matrix products  60.8 us (7%)
  other arithmetic  30.5 us (4%)
  starting transfers between devices  27.7 us (3%)
  between operations  15.2 us (2%)
    unnamed x5, waiting for transfers between devices  218 us
    pmax x3, waiting for transfers between devices, by_axis(): return functools.reduce(lax.pmax, axes, x)  192 us
    all_to_all x1, waiting for transfers between devices, _fit_sites(): taken_in = lax.all_to_all(built, KV, 0, 0)  110 us
    pmax x3, blocking collectives, by_axis(): return functools.reduce(lax.pmax, axes, x)  75.3 us
    all_to_all x1, starting transfers between devices, _fit_sites(): taken_in = lax.all_to_all(built, KV, 0, 0)  27.1 us
    unnamed x49, local copies, waits for them, and re-layouts  26.9 us
    dot_general x8, matrix products, per_device(): jnp.einsum('qhd,khd->hqk', sub_block, ckeys, preferred_element_type=jnp.f...  24.8 us
    dot_general x8, matrix products, per_device(): jnp.einsum('hqk,khd->qhd', cache_weight.astype(jnp.bfloat16), cache_value...  21.2 us
  transfers between devices with their start and end apart: 5, of which 5 were waited for; matrix products, arithmetic and copies ran while one was open for 3% of the time, Pallas kernels for 0%

profile of v1, /device:TPU:518, one launch (start us, length us, event | category | flops | bytes accessed | tf_op | source)
XLA Modules:
  0.0 816.5 jit_solution(18286239357051047641)
XLA Ops:
  6.5 3.8 stack.2
  10.4 27.1 %all-to-all-start = ((bf16[128,4,40,128]{3,2,1,0:T(8,128)(2,1)}), bf16[128,4,40,128]{3,2,1,0:T(8,128)(2,1)}, u32[]{:S(2)}, u32[]{:S(2)}) async-start(bf16[128,4,40,128]{3,2,1,0:T(8,128)(2,1)} %stack.2), calls=%async_computation | async-start | bytes 10485760 | tf_op jit(solution)/shard_map/all_to_all | solution.py:47
  38.5 2.5 fusion.168
  43.1 2.1 copy.42
  45.3 4.3 fusion.169
  49.6 109.9 %all-to-all-done = bf16[128,4,40,128]{3,2,1,0:T(8,128)(2,1)} async-done(((bf16[128,4,40,128]{3,2,1,0:T(8,128)(2,1)}), bf16[128,4,40,128]{3,2,1,0:T(8,128)(2,1)}, u32[]{:S(2)}, u32[]{:S(2)}) %all-to-all-start) | async-done | bytes 5242912 | tf_op jit(solution)/shard_map/all_to_all | solution.py:47
  159.5 4.6 copy.125
  164.1 2.4 fusion.67
  180.2 2.1 fusion
  182.4 33.6 %pmax.168 = f32[20,128]{1,0:T(8,128)S(1)} all-reduce(f32[20,128]{1,0:T(8,128)S(1)} %max.72), channel_id=1, replica_groups=mesh['grp'=2,'kv_0'=8,'kv_1'=8,'kv_2'=2] {'kv_0'}, use_global_device_ids=true, to_apply=%region_2.3 | all-reduce | flops 2560 | bytes 20480 | tf_op jit(solution)/shard_map/pmax | solution.py:17
  216.0 26.6 %pmax.169 = f32[20,128]{1,0:T(8,128)S(1)} all-reduce(f32[20,128]{1,0:T(8,128)S(1)} %pmax.168), channel_id=1, replica_groups=mesh['grp'=2,'kv_0'=8,'kv_1'=8,'kv_2'=2] {'kv_1'}, use_global_device_ids=true, to_apply=%region_3.4 | all-reduce | flops 2560 | bytes 20480 | tf_op jit(solution)/shard_map/pmax | solution.py:17
  242.7 15.0 %pmax.170 = f32[20,128]{1,0:T(8,128)S(1)} all-reduce(f32[20,128]{1,0:T(8,128)S(1)} %pmax.169), channel_id=1, replica_groups=mesh['grp'=2,'kv_0'=8,'kv_1'=8,'kv_2'=2] {'kv_2'}, use_global_device_ids=true, to_apply=%region_4.5 | all-reduce | flops 2560 | bytes 20480 | tf_op jit(solution)/shard_map/pmax | solution.py:17
  257.7 10.3 %fusion.8 = (f32[20,128]{1,0:T(8,128)S(1)}, f32[20,128]{1,0:T(8,128)S(1)}, f32[20,128]{1,0:T(8,128)S(1)}, f32[20,128]{1,0:T(8,128)S(1)}, f32[20,128]{1,0:T(8,128...) fusion(f32[20,128,256]{2,1,0:T(8,128)} %get-tuple-element.58, ...), kind=kOutput, calls=%fused_computation.25 | convolution fusion | flops 184135680 | bytes 23947520 | tf_op jit(solution)/shard_map/qhd,khd->hqk/dot_general | solution.py:68
  272.6 3.6 convolution_add_fusion.7
  276.3 89.4 %all-reduce.29.cloned.1.call-done = (f32[20,128]{1,0:T(8,128)}, f32[20,128]{1,0:T(8,128)}, f32[20,128]{1,0:T(8,128)}, f32[20,128]{1,0:T(8,128)}, f32[20,128]{1,0...) async-done(((f32[20,128]{1,0:T(8,128)}, f32[20,128]{1,0:T(8,128)}, f32[20,128]{1,0:T(8,128)}, f32[20,128]{1,0:T(8,128)}, f32[20,128]{1,0:T(8,128)}, ...) | async-done | bytes 71696 | tf_op jit(solution)/shard_map/pmax | solution.py:17
  365.9 77.3 %all-reduce.27.cloned.1.call-done = (f32[20,128]{1,0:T(8,128)}, f32[20,128]{1,0:T(8,128)}, f32[20,128]{1,0:T(8,128)}, f32[20,128]{1,0:T(8,128)}, f32[20,128]{1,0...) async-done(((f32[20,128]{1,0:T(8,128)}, f32[20,128]{1,0:T(8,128)}, f32[20,128]{1,0:T(8,128)}, f32[20,128]{1,0:T(8,128)}, f32[20,128]{1,0:T(8,128)}, ...) | async-done | bytes 71696 | tf_op jit(solution)/shard_map/pmax | solution.py:17
  443.3 2.5 pad_maximum_fusion
  445.8 2.8 copy.48
  448.6 2.6 pad.25.clone
  451.3 2.6 reshape.129
  453.8 25.0 %all-reduce.31.cloned.1.call-done = (f32[20,128]{1,0:T(8,128)}, f32[20,128]{1,0:T(8,128)}, f32[20,128]{1,0:T(8,128)}, f32[20,128]{1,0:T(8,128)}, f32[20,128]{1,0...) async-done(((f32[20,128]{1,0:T(8,128)}, f32[20,128]{1,0:T(8,128)}, f32[20,128]{1,0:T(8,128)}, f32[20,128]{1,0:T(8,128)}, f32[20,128]{1,0:T(8,128)}, ...) | async-done | bytes 71696 | tf_op jit(solution)/shard_map/pmax | solution.py:17
  480.8 2.3 fusion.98
  490.8 8.7 %fusion.10 = (f32[20,128]{1,0:T(8,128)S(1)}, f32[20,128]{1,0:T(8,128)S(1)}, f32[20,128]{1,0:T(8,128)S(1)}, f32[20,128]{1,0:T(8,128)S(1)}, f32[20,128]{1,0:T(8,12...) fusion(f32[20,128,256]{2,1,0:T(8,128)} %get-tuple-element.61, f32[20,128]{1,0:T(8,128)S(1)} %copy-done.9, ...), kind=kLoop, calls=%fused_computation.27 | loop fusion | flops 18332160 | bytes 18493696 | tf_op jit(solution)/shard_map/reduce_sum | solution.py:84
  501.5 2.8 copy.55
  504.3 2.6 pad.32.clone
  506.9 2.6 reshape.143
  509.5 2.9 convolution_add_fusion.1
  513.5 2.9 copy.54
  516.4 2.6 pad.31.clone
  519.0 2.5 reshape.141
  521.6 2.9 convolution_add_fusion.2
  525.6 2.8 copy.53
  528.5 2.7 pad.30.clone
  531.2 2.6 reshape.139
  533.7 2.9 convolution_add_fusion.3
  537.8 2.9 copy.52
  540.6 2.7 pad.29.clone
  543.3 2.6 reshape.137
  545.9 2.9 convolution_add_fusion.4
  550.0 2.9 copy.51
  552.8 2.7 pad.28.clone
  555.5 2.6 reshape.135
  558.1 2.9 convolution_add_fusion.5
  562.1 2.9 copy.50
  565.0 2.7 pad.27.clone
  567.7 2.7 reshape.133
  570.5 2.5 convolution_add_fusion.6
  579.5 217.5 %all-reduce.25.cloned.1.call-done = (f32[3072,128]{1,0:T(8,128)}, f32[3072,128]{1,0:T(8,128)}, f32[3072,128]{1,0:T(8,128)}, f32[3072,128]{1,0:T(8,128)}, f32[307...) async-done(((f32[3072,128]{1,0:T(8,128)}, f32[3072,128]{1,0:T(8,128)}, f32[3072,128]{1,0:T(8,128)}, f32[3072,128]{1,0:T(8,128)}, ...) | async-done | bytes 12582928
  (128 shorter events, 57.1 us)
Async XLA Ops:
  10.3 28.2 %copy-start.6 = (bf16[256,40,128]{2,1,0:T(8,128)(2,1)S(1)}, bf16[256,40,128]{2,1,0:T(8,128)(2,1)}, u32[]{:S(2)}) copy-start(bf16[256,40,128]{2,1,0:T(8,128)(2,1)} %param.8) | copy-start | bytes 7864324
  10.4 149.1 %all-to-all-start = ((bf16[128,4,40,128]{3,2,1,0:T(8,128)(2,1)}), bf16[128,4,40,128]{3,2,1,0:T(8,128)(2,1)}, u32[]{:S(2)}, u32[]{:S(2)}) async-start(bf16[128,4,40,128]{3,2,1,0:T(8,128)(2,1)} %stack.2), calls=%async_computation | async-start | bytes 10485760 | tf_op jit(solution)/shard_map/all_to_all | solution.py:47
  37.4 328.3 %all-reduce.29.cloned.1.call-start = ((), (), s32[]{:S(2)}) async-start(), calls=%async_computation.3 | async-start | bytes 172032 | tf_op jit(solution)/shard_map/pmax | solution.py:17
  43.1 2.1 copy-start.16
  43.1 2.1 copy-start.17
  159.5 4.6 copy-start.8
  164.1 16.1 %copy-start = (bf16[128,4,40,128]{3,0,2,1:T(8,128)(2,1)}, bf16[128,4,40,128]{3,0,2,1:T(8,128)(2,1)S(1)}, u32[]{:S(2)}) copy-start(bf16[128,4,40,128]{3,0,2,1:T(8,128)(2,1)S(1)} %copy.125) | copy-start | bytes 15728644
  166.5 2.0 copy-start.7
  276.2 167.0 %all-reduce.27.cloned.1.call-start = ((), (), s32[]{:S(2)}) async-start(), calls=%async_computation.2 | async-start | bytes 172032 | tf_op jit(solution)/shard_map/pmax | solution.py:17
  365.8 113.1 %all-reduce.31.cloned.1.call-start = ((), (), s32[]{:S(2)}) async-start(), calls=%async_computation.4 | async-start | bytes 172032 | tf_op jit(solution)/shard_map/pmax | solution.py:17
  443.2 353.7 %all-reduce.25.cloned.1.call-start = ((), (), s32[]{:S(2)}) async-start(), calls=%async_computation.1 | async-start | bytes 25165824
  478.9 4.2 copy-start.13
  478.9 4.2 copy-start.14
  480.8 3.9 copy-start.12
  480.8 10.0 %copy-start.3 = (f32[20,128,256]{2,1,0:T(8,128)S(1)}, f32[20,128,256]{2,1,0:T(8,128)}, u32[]{:S(2)}) copy-start(f32[20,128,256]{2,1,0:T(8,128)} %fusion.69) | copy-start | bytes 7864324
  483.1 3.1 copy-start.11
  484.7 3.0 copy-start.10
  484.7 6.1 copy-start.2
  486.1 3.1 copy-start.9
  487.7 3.1 copy-start.1
  487.7 3.1 copy-start.15
  490.8 8.7 %copy-start.4 = (f32[20,128,256]{2,1,0:T(8,128)S(1)}, f32[20,128,256]{2,1,0:T(8,128)}, u32[]{:S(2)}) copy-start(f32[20,128,256]{2,1,0:T(8,128)} %fusion.70) | copy-start | bytes 7864324
  567.7 2.7 copy-start.5
  577.6 0.7 copy-start.18
Sparse Core Ops, SparseCore 0:
  276.3 89.3 all-reduce.28
  368.6 74.4 all-reduce.26
  446.3 32.5 all-reduce.30
  577.7 219.1 all-reduce.24
